TPU v7x, 32 devices: a whole 2x2x4 slice. The times are simulated.
32 devices in a mesh: seq: 4 (over y, core), tp: 8 (over z, x).
Axes of the slice: x: 2, y: 2, z: 4, core: 2. Of those that a mesh axis runs over, the one named last changes fastest.
Arguments:
- tokens: bfloat16 [4096, 5376], P('seq'), may hold values from -6 to 6
- pre_gain: float32 [5376], replicated, may hold values from 0.5 to 2
- w_query: bfloat16 [5376, 4096], P(None, 'tp'), may hold values from -0.078125 to 0.078125
- key_weight_matrix: bfloat16 [5376, 2048], P(None, 'tp'), may hold values from -0.078125 to 0.078125
- value_weight_matrix: bfloat16 [5376, 2048], P(None, 'tp'), may hold values from -0.078125 to 0.078125
- query_gain: float32 [128], replicated, may hold values from 0.5 to 9
- key_norm_gain: float32 [128], replicated, may hold values from 0.5 to 9
- prior_key_cache: bfloat16 [1024, 2048], P(None, 'tp'), may hold values from -6 to 6
- prior_value_cache: bfloat16 [1024, 2048], P(None, 'tp'), may hold values from -6 to 6
- w_out: bfloat16 [4096, 5376], P('tp'), may hold values from -0.09375 to 0.09375
- post_gain: float32 [5376], replicated, may hold values from 0.5 to 2
Outputs:
- updated: bfloat16 [4096, 5376], P(('seq', 'tp'))
All inputs are finite; a program needn't handle non-finite values.
Results may differ from a plain program's by a relative error of at most 0.015.
The roundings to bfloat16 on the way count: a program that leaves them out, or rounds other values in their place, can miss the bound.
Values may be sent and summed in bfloat16 or wider, within the bound.
A program may use at most 128 MiB of HBM per device.

v0:
```python
import jax
import jax.numpy as jnp
from jax import lax
from jax.sharding import PartitionSpec as P

MODEL_WIDTH = 5376
HQ = 32
WINDOW_SPAN = 1024


EPSILON = 1e-06


def shifted(value, axis, steps):
    count = lax.axis_size(axis)
    first, last = (max(0, -steps), min(count, count - steps))
    return lax.ppermute(value, axis, [(source, source + steps) for source in range(first, last)])


def root_mean_norm(values, gain):
    mean_square = jnp.mean(values * values, axis=-1, keepdims=True)
    return values * lax.rsqrt(mean_square + EPSILON) * gain


def rotary_embed_pairs(values, token_positions):
    half = values.shape[-1] // 2
    exponent = jnp.arange(half, dtype=jnp.float32) * (-2.0 / values.shape[-1])
    frequency = jnp.power(jnp.float32(10000.0), exponent)
    angles = token_positions.astype(jnp.float32)[:, None] * frequency[None, :]
    cosine = jnp.cos(angles)[:, None, :]
    sine = jnp.sin(angles)[:, None, :]
    first = values[..., :half]
    second = values[..., half:]
    return jnp.concatenate(
        [first * cosine - second * sine, second * cosine + first * sine], axis=-1
    )


def attend_block(query_rows, key_rows, value_rows, scale):
    count = query_rows.shape[0]
    heads = query_rows.shape[1]
    kv_heads = key_rows.shape[1]
    grouped = query_rows.reshape(count, kv_heads, heads // kv_heads, -1)
    scores = (
        jnp.einsum("bkgd,mkd->kgbm", grouped, key_rows, preferred_element_type=jnp.float32) * scale
    )
    row_ids = lax.broadcasted_iota(jnp.int32, (count, key_rows.shape[0]), 0)
    col_ids = lax.broadcasted_iota(jnp.int32, (count, key_rows.shape[0]), 1)
    allowed = (col_ids > row_ids) & (col_ids <= row_ids + WINDOW_SPAN)
    scores = jnp.where(allowed, scores, -jnp.inf)
    highest = jnp.max(scores, axis=-1, keepdims=True)
    weights = jnp.exp(scores - highest)
    weights = (weights / jnp.sum(weights, axis=-1, keepdims=True)).astype(jnp.bfloat16)
    mixed = jnp.einsum("kgbm,mkd->bkgd", weights, value_rows, preferred_element_type=jnp.float32)
    return mixed.astype(jnp.bfloat16).reshape(count, heads, -1)


def per_device(
    tokens,
    pre_gain,
    w_query,
    key_weight_matrix,
    value_weight_matrix,
    query_gain,
    key_norm_gain,
    prior_key_cache,
    prior_value_cache,
    w_out,
    post_gain,
):
    seq_tokens = tokens.shape[0]
    local_rows = seq_tokens // lax.axis_size("tp")
    head_size = query_gain.shape[0]
    query_cols = w_query.shape[1]
    key_cols = key_weight_matrix.shape[1]
    normed = root_mean_norm(tokens.astype(jnp.float32), pre_gain).astype(jnp.bfloat16)
    query_raw = jnp.dot(normed, w_query, preferred_element_type=jnp.float32)
    unnormed_keys = jnp.dot(normed, key_weight_matrix, preferred_element_type=jnp.float32)
    projected_values = jnp.dot(normed, value_weight_matrix, preferred_element_type=jnp.float32)
    seq_index = lax.axis_index("seq")
    token_positions = WINDOW_SPAN + seq_index * seq_tokens + jnp.arange(seq_tokens, dtype=jnp.int32)
    queries = rotary_embed_pairs(
        root_mean_norm(query_raw.reshape(seq_tokens, -1, head_size), query_gain), token_positions
    ).astype(jnp.bfloat16)
    block_keys = rotary_embed_pairs(
        root_mean_norm(unnormed_keys.reshape(seq_tokens, -1, head_size), key_norm_gain),
        token_positions,
    ).astype(jnp.bfloat16)
    key_flat = block_keys.reshape(seq_tokens, key_cols)
    value_flat = projected_values.astype(jnp.bfloat16)
    got_keys, got_values = shifted((key_flat, value_flat), "seq", 1)
    source = seq_index - 1
    present = source >= 0
    key_parts = [jnp.where(present, got_keys, prior_key_cache)]
    value_parts = [jnp.where(present, got_values, prior_value_cache)]
    context_keys = jnp.concatenate(key_parts + [key_flat], axis=0)
    context_values = jnp.concatenate(value_parts + [value_flat], axis=0)
    context_keys = context_keys.reshape(WINDOW_SPAN + seq_tokens, -1, head_size)
    context_values = context_values.reshape(WINDOW_SPAN + seq_tokens, -1, head_size)
    size = min(512, seq_tokens)
    scale = float(MODEL_WIDTH // HQ) ** (-0.5)
    outputs = []
    for number in range(seq_tokens // size):
        first_row = number * size
        outputs.append(
            attend_block(
                queries[first_row : first_row + size],
                context_keys[first_row : first_row + size + WINDOW_SPAN],
                context_values[first_row : first_row + size + WINDOW_SPAN],
                scale,
            )
        )
    attended = jnp.concatenate(outputs, axis=0).reshape(seq_tokens, query_cols)
    partial_value = jnp.dot(attended, w_out, preferred_element_type=jnp.float32)
    summed = lax.psum_scatter(
        partial_value.astype(jnp.bfloat16), "tp", scatter_dimension=0, tiled=True
    ).astype(jnp.float32)
    own_start = lax.axis_index("tp") * local_rows
    own_rows = lax.dynamic_slice_in_dim(tokens, own_start, local_rows, 0).astype(jnp.float32)
    return (own_rows + root_mean_norm(summed, post_gain)).astype(jnp.bfloat16)


def solution(mesh):
    return jax.shard_map(
        per_device,
        mesh=mesh,
        in_specs=(
            P("seq", None),
            P(),
            P(None, "tp"),
            P(None, "tp"),
            P(None, "tp"),
            P(),
            P(),
            P(None, "tp"),
            P(None, "tp"),
            P("tp", None),
            P(),
        ),
        out_specs=P(("seq", "tp"), None),
        check_vma=False,
    )
```

profile of v0, /device:TPU:0, one launch (start us, length us, event | category | flops | bytes accessed | tf_op | source)
XLA Modules:
  0.0 297.9 jit_solution(8082281493998134321)
XLA Ops:
  6.5 0.0 copy-start
  6.5 0.0 reduce-scatter.2.cloned.1.call-start
  6.6 6.5 %fusion.2 = f32[1024]{0:T(1024)S(1)} fusion(bf16[1024,5376]{1,0:T(8,128)(2,1)} %param.11), kind=kLoop, calls=%fused_computation.4 | loop fusion | flops 16514048 | bytes 11014144 | tf_op jit(solution)/shard_map/reduce_sum | solution.py:21
  13.0 0.0 copy-done
  13.1 0.0 copy-start.8
  13.1 8.5 %multiply_reduce_fusion.1 = (f32[1024,2]{0,1:T(2,128)S(1)}, f32[1024,256]{0,1:T(8,128)}) fusion(bf16[5376,256]{1,0:T(8,128)(2,1)S(1)} %copy-done, bf16[1024,5376]{1,0:T(8,128)(2,1)} %param.11, f32[5376]{0:T(1024)S(1)} %copy-done.10, f32[1024]{0:T(1024)S(1)} %add_rsqrt_fusion.2), kind=kOutput, calls=%fused_computation.52 | convolution fusion | flops 2841114624 | bytes 14844928 | tf_op jit(solution)/shard_map/dot_general | solution.py:78
  21.6 1.0 multiply_cosine_fusion
  22.6 1.4 multiply_multiply_fusion.1
  23.9 0.2 subtract_convert_fusion.1
  24.2 0.2 copy.39
  24.4 3.2 %collective-permute-start.1 = (bf16[1024,256]{1,0:T(8,128)(2,1)S(1)}, bf16[1024,256]{1,0:T(8,128)(2,1)}, u32[]{:S(2)}, u32[]{:S(2)}) collective-permute-start(bf16[1024,256]{1,0:T(8,128)(2,1)S(1)} %copy.39), channel_id=1, source_target_pairs={{0,8},{8,16},{16,24},{1,9},{9,17},{17,25},{2,10},{10,18},{18,26},{... | collective-permute-start | bytes 1572872 | tf_op jit(solution)/shard_map/ppermute | solution.py:17
  27.6 8.0 %convolution_convert_fusion.1 = bf16[1024,256]{1,0:T(8,128)(2,1)S(1)} fusion(bf16[5376,256]{1,0:T(8,128)(2,1)} %param.15, bf16[1024,5376]{1,0:T(8,128)(2,1)} %param.11, f32[5376]{0:T(1024)S(1)} %copy-done.10, f32[1024]{0:T(1024)S(1)} %add_rsqrt_fusion.2), kind=kOutput, calls=%fused_computation.39 | convolution fusion | flops 2840854528 | bytes 14312448 | tf_op jit(solution)/shard_map/dot_general | solution.py:79
  35.6 0.0 copy-start.5
  35.6 0.0 copy-start.9
  35.6 4.7 %collective-permute-start = (bf16[1024,256]{1,0:T(8,128)(2,1)S(1)}, bf16[1024,256]{1,0:T(8,128)(2,1)}, u32[]{:S(2)}, u32[]{:S(2)}) collective-permute-start(bf16[1024,256]{1,0:T(8,128)(2,1)S(1)} %convolution_convert_fusion.1), channel_id=1, source_target_pairs={{0,8},{8,16},{16,24},{1,9},{9,17},{17,25},{2,10},{10,18},{18,26},{... | collective-permute-start | bytes 1572872 | tf_op jit(solution)/shard_map/ppermute | solution.py:17
  40.3 10.8 %multiply_reduce_fusion = (f32[1024,4]{0,1:T(4,128)S(1)}, f32[1024,512]{0,1:T(8,128)S(1)}) fusion(bf16[5376,512]{1,0:T(8,128)(2,1)} %param.13, bf16[1024,5376]{1,0:T(8,128)(2,1)} %param.11, f32[5376]{0:T(1024)S(1)} %copy-done.10, f32[1024]{0:T(1024)S(1)} %add_rsqrt_fusion.2), kind=kOutput, calls=%fused_computation.34 | convolution fusion | flops 5660209152 | bytes 18654208 | tf_op jit(solution)/shard_map/dot_general | solution.py:77
  51.1 0.0 copy-start.6
  51.1 0.4 multiply_multiply_fusion
  51.6 0.4 subtract_convert_fusion
  51.9 1.1 fusion.45
  53.0 1.4 fusion.15
  54.4 0.0 collective-permute-done.1
  54.4 0.0 collective-permute-done
  54.5 1.2 broadcast_select_fusion
  55.6 0.1 fusion.29
  55.7 1.1 slice.47
  56.9 1.2 fusion.30
  58.1 1.2 copy.38
  59.3 1.1 slice.54
  60.3 0.3 copy.42
  60.6 0.0 copy-start.2
  60.6 10.7 %fusion.61 = (f32[2,2,512]{2,1,0:T(2,128)S(1)}, f32[2,2,512,1536]{2,3,1,0:T(8,128)}) fusion(pred[512,1536]{0,1:T(8,128)(4,1)} %fusion.15, bf16[512,2,2,128]{0,3,2,1:T(8,128)(2,1)} %bitcast.67, bf16[1536,2,128,1]{2,1,0,3:T(2,128)(2,1)} %bitcast.64), kind=kOutput, calls=%fused_computation.87 | convolution fusion | flops 817890816 | bytes 14688256 | tf_op jit(solution)/shard_map/sub | solution.py:52
  71.3 0.0 copy-done.4
  71.3 0.0 copy-start.3
  71.4 10.1 %fusion.56 = (f32[2,2,512]{2,1,0:T(2,128)S(1)}, f32[2,2,512,1536]{2,3,1,0:T(8,128)}) fusion(pred[512,1536]{0,1:T(8,128)(4,1)S(1)} %copy-done.2, bf16[512,2,2,128]{0,3,2,1:T(8,128)(2,1)} %bitcast.66, bf16[1536,2,128,1]{2,1,0,3:T(2,128)(2,1)S(1)} %bitcast.65), kind=kOutput, calls=%fused_computation.86 | convolution fusion | flops 817890816 | bytes 14688256 | tf_op jit(solution)/shard_map/sub | solution.py:52
  81.4 0.0 copy-done.3
  81.4 6.0 %fusion.25 = bf16[2,128,2,512]{3,1,2,0:T(8,128)(2,1)S(1)} fusion(bf16[1536,2,128,1]{0,2,3,1:T(8,128)(2,1)S(1)} %bitcast.62, f32[2,2,512,1536]{2,3,1,0:T(8,128)} %get-tuple-element.24, f32[2,2,512]{2,1,0:T(2,128)S(1)} %get-tuple-element.23), kind=kOutput, calls=%fused_computation.38 | convolution fusion | flops 811859968 | bytes 13901824 | tf_op jit(solution)/shard_map/kgbm,mkd->bkgd/dot_general | solution.py:54
  87.4 0.0 slice-start.1
  87.4 2.2 copy-done.11
  89.6 1.0 fusion.24
  90.6 0.2 slice-done
  90.8 0.6 slice-done.1
  91.3 8.6 %convolution_convert_fusion = bf16[1024,5376]{1,0:T(8,128)(2,1)} fusion(bf16[512,5376]{1,0:T(8,128)(2,1)S(1)} %bitcast.69, bf16[512,512]{0,1:T(8,128)(2,1)S(1)} %bitcast.71, bf16[512,512]{0,1:T(8,128)(2,1)S(1)} %bitcast.70), kind=kOutput, calls=%fused_computation.13 | convolution fusion | flops 5644746752 | bytes 17563648 | tf_op jit(solution)/shard_map/dot_general | solution.py:114
  100.0 0.0 reduce-scatter.2.cloned.1.call-update
  100.0 186.0 %reduce-scatter.2.cloned.1.call-done = bf16[128,5376]{1,0:T(8,128)(2,1)} async-done(((bf16[1024,5376]{1,0:T(8,128)(2,1)}), bf16[128,5376]{1,0:T(8,128)(2,1)}) %reduce-scatter.2.cloned.1.call-update) | async-done | bytes 1376272 | tf_op jit(solution)/shard_map/reduce_scatter | solution.py:115
  286.0 1.7 fusion.16
  287.7 3.4 %fusion.19 = bf16[128,5376]{1,0:T(8,128)(2,1)} fusion(bf16[128,5376]{1,0:T(8,128)(2,1)} %reduce-scatter.2.cloned.1.call-done, f32[5376]{0:T(1024)S(1)} %copy-done.7, f32[128]{0:T(128)S(1)} %add_rsqrt_fusion.3, bf16[1024,5376]{1,0:T(8,128)(2,1)} %param.11, s32[]{:T(128)S(6)} %select_n.22), kind=kLoop, calls=%fused_computation.32 | loop fusion | flops 4128768 | bytes 4150788 | tf_op jit(solution)/shard_map/convert_element_type | solution.py:120
  291.1 0.0 copy-done.1
  (22 shorter events, 0.1 us)
Async XLA Ops:
  6.5 6.5 %copy-start = (bf16[5376,256]{1,0:T(8,128)(2,1)S(1)}, bf16[5376,256]{1,0:T(8,128)(2,1)}, u32[]{:S(2)}) copy-start(bf16[5376,256]{1,0:T(8,128)(2,1)} %param.14) | copy-start | bytes 8257540
  6.5 6.5 %copy-start.10 = (f32[5376]{0:T(1024)S(1)}, f32[5376]{0:T(1024)}, u32[]{:S(2)}) copy-start(f32[5376]{0:T(1024)} %param.12) | copy-start | bytes 64516
  6.5 279.4 %reduce-scatter.2.cloned.1.call-start = ((), (), s32[]{:S(2)}) async-start(), calls=%async_computation.1 | async-start | bytes 12386304 | tf_op jit(solution)/shard_map/reduce_scatter | solution.py:115
  13.1 9.5 %copy-start.8 = (f32[128]{0:T(128)S(1)}, f32[128]{0:T(128)}, u32[]{:S(2)}) copy-start(f32[128]{0:T(128)} %param.17) | copy-start | bytes 1540
  24.4 30.1 %collective-permute-start.1 = (bf16[1024,256]{1,0:T(8,128)(2,1)S(1)}, bf16[1024,256]{1,0:T(8,128)(2,1)}, u32[]{:S(2)}, u32[]{:S(2)}) collective-permute-start(bf16[1024,256]{1,0:T(8,128)(2,1)S(1)} %copy.39), channel_id=1, source_target_pairs={{0,8},{8,16},{16,24},{1,9},{9,17},{17,25},{2,10},{10,18},{18,26},{... | collective-permute-start | bytes 1572872 | tf_op jit(solution)/shard_map/ppermute | solution.py:17
  35.6 15.5 %copy-start.5 = (bf16[1024,256]{1,0:T(8,128)(2,1)}, bf16[1024,256]{1,0:T(8,128)(2,1)S(1)}, u32[]{:S(2)}) copy-start(bf16[1024,256]{1,0:T(8,128)(2,1)S(1)} %convolution_convert_fusion.1) | copy-start | bytes 1572868
  35.6 15.5 %copy-start.9 = (f32[128]{0:T(128)S(1)}, f32[128]{0:T(128)}, u32[]{:S(2)}) copy-start(f32[128]{0:T(128)} %param.16) | copy-start | bytes 1540
  35.6 18.8 %collective-permute-start = (bf16[1024,256]{1,0:T(8,128)(2,1)S(1)}, bf16[1024,256]{1,0:T(8,128)(2,1)}, u32[]{:S(2)}, u32[]{:S(2)}) collective-permute-start(bf16[1024,256]{1,0:T(8,128)(2,1)S(1)} %convolution_convert_fusion.1), channel_id=1, source_target_pairs={{0,8},{8,16},{16,24},{1,9},{9,17},{17,25},{2,10},{10,18},{18,26},{... | collective-permute-start | bytes 1572872 | tf_op jit(solution)/shard_map/ppermute | solution.py:17
  51.1 3.4 %copy-start.6 = (bf16[1024,256]{1,0:T(8,128)(2,1)S(1)}, bf16[1024,256]{1,0:T(8,128)(2,1)}, u32[]{:S(2)}) copy-start(bf16[1024,256]{1,0:T(8,128)(2,1)} %param.18) | copy-start | bytes 1572868
  60.6 10.7 %copy-start.2 = (pred[512,1536]{0,1:T(8,128)(4,1)S(1)}, pred[512,1536]{0,1:T(8,128)(4,1)}, u32[]{:S(2)}) copy-start(pred[512,1536]{0,1:T(8,128)(4,1)} %fusion.15) | copy-start | bytes 2359300
  60.6 10.7 %copy-start.4 = (bf16[1536,2,128]{2,1,0:T(2,128)(2,1)S(1)}, bf16[1536,2,128]{2,1,0:T(2,128)(2,1)}, u32[]{:S(2)}) copy-start(bf16[1536,2,128]{2,1,0:T(2,128)(2,1)} %slice.54) | copy-start | bytes 2359300
  71.3 10.1 %copy-start.3 = (bf16[1536,256]{0,1:T(8,128)(2,1)S(1)}, bf16[1536,256]{0,1:T(8,128)(2,1)}, u32[]{:S(2)}) copy-start(bf16[1536,256]{0,1:T(8,128)(2,1)} %copy.38) | copy-start | bytes 2359300
  81.4 8.2 %copy-start.11 = (f32[2,2,512,1536]{2,3,1,0:T(8,128)S(1)}, f32[2,2,512,1536]{2,3,1,0:T(8,128)}, u32[]{:S(2)}) copy-start(f32[2,2,512,1536]{2,3,1,0:T(8,128)} %get-tuple-element.22) | copy-start | bytes 37748740
  81.4 9.3 %slice-start = ((s8[5505024]{0:T(1024)(128)(4,1)}), s8[4194304]{0:T(1024)(128)(4,1)S(1)}, s32[]{:S(2)}) async-start(s8[5505024]{0:T(1024)(128)(4,1)} %bitcast.68), calls=%async_computation.2 | async-start | bytes 8388608
  87.4 3.9 %slice-start.1 = ((s8[5505024]{0:T(1024)(128)(4,1)}), s8[1310720]{0:T(1024)(128)(4,1)S(1)}, s32[]{:S(2)}) async-start(s8[5505024]{0:T(1024)(128)(4,1)} %bitcast.68), calls=%async_computation.3 | async-start | bytes 2621440
  100.0 187.7 %copy-start.7 = (f32[5376]{0:T(1024)S(1)}, f32[5376]{0:T(1024)}, u32[]{:S(2)}) copy-start(f32[5376]{0:T(1024)} %param.21) | copy-start | bytes 64516
  100.0 191.1 %copy-start.1 = (bf16[5376,256]{1,0:T(8,128)(2,1)S(1)}, bf16[5376,256]{1,0:T(8,128)(2,1)}, u32[]{:S(2)}) copy-start(bf16[5376,256]{1,0:T(8,128)(2,1)} %param.14) | copy-start | bytes 8257540
Sparse Core Ops, SparseCore 0:
  100.1 185.7 reduce-scatter.1
where the time goes:
time: 298 us
  waiting for transfers between devices  186 us (62%)
  matrix products  63.6 us (21%)
  other arithmetic  20 us (7%)
  between operations  13.7 us (5%)
  starting transfers between devices  7.9 us (3%)
  local copies, waits for them, and re-layouts  6.82 us (2%)
    reduce_scatter x1, waiting for transfers between devices, per_device(): lax.psum_scatter(partial_value.astype(jnp.bfloat16), 'tp', scatter_dimens...  186 us
    sub x2, matrix products, attend_block(): weights = jnp.exp(scores - highest)  20.8 us
    dot_general x1, matrix products, per_device(): query_raw = jnp.dot(normed, w_query, preferred_element_type=jnp.float32)  10.8 us
    dot_general x1, matrix products, per_device(): partial_value = jnp.dot(attended, w_out, preferred_element_type=jnp.float32)  8.64 us
    dot_general x1, matrix products, per_device(): jnp.dot(normed, key_weight_matrix, preferred_element_type=jnp.float32)  8.47 us
    reduce_sum x2, other arithmetic, root_mean_norm(): mean_square = jnp.mean(values * values, axis=-1, keepdims=True)  8.17 us
    dot_general x1, matrix products, per_device(): jnp.dot(normed, value_weight_matrix, preferred_element_type=jnp.float32)  7.97 us
    ppermute x2, starting transfers between devices, shifted(): lax.ppermute(value, axis, [(source, source + steps) for source in range(f...  7.9 us
  transfers between devices with their start and end apart: 3, of which 1 were waited for; matrix products, arithmetic and copies ran while one was open for 7% of the time, Pallas kernels for 0%

commit v1 on v0

v1 whole, which is shorter than its diff:
```python
import functools

import jax
import jax.numpy as jnp
from jax import lax
from jax.experimental import pallas as pl
from jax.experimental.pallas import tpu as pltpu
from jax.sharding import PartitionSpec as P


MODEL_WIDTH = 5376
HQ = 32
WINDOW_SPAN = 1024


EPSILON = 1e-06


def shifted(value, axis, steps):
    count = lax.axis_size(axis)
    first, last = (max(0, -steps), min(count, count - steps))
    return lax.ppermute(value, axis, [(source, source + steps) for source in range(first, last)])


def swapped(value, axis, bit):
    count = lax.axis_size(axis)
    return lax.ppermute(value, axis, [(source, source ^ bit) for source in range(count)])


def turned(value, axis, steps):
    count = lax.axis_size(axis)
    return lax.ppermute(
        value, axis, [(source, (source + steps) % count) for source in range(count)]
    )


def root_mean_norm(values, gain):
    mean_square = jnp.mean(values * values, axis=-1, keepdims=True)
    return values * lax.rsqrt(mean_square + EPSILON) * gain


def rotary_tables(half, token_positions):
    exponent = jnp.arange(half, dtype=jnp.float32) * (-1.0 / half)
    frequency = jnp.power(jnp.float32(10000.0), exponent)
    angles = token_positions.astype(jnp.float32)[:, None] * frequency[None, :]
    return jnp.cos(angles), jnp.sin(angles)


def project_kernel(head_size, kinds, x_ref, w_ref, gain_ref, cos_ref, sin_ref, out_ref):
    raw = jnp.dot(x_ref[...], w_ref[...], preferred_element_type=jnp.float32)
    if not kinds:
        out_ref[...] = raw.astype(out_ref.dtype)
        return
    half = head_size // 2
    gain = gain_ref[...]
    cosine = cos_ref[...]
    sine = sin_ref[...]
    for head in range(raw.shape[1] // head_size):
        u = raw[:, head * head_size : (head + 1) * head_size]
        mean_square = jnp.mean(u * u, axis=-1, keepdims=True)
        u = u * lax.rsqrt(mean_square + EPSILON) * gain
        turned_u = pltpu.roll(u, half, 1)
        out_ref[:, head * head_size : (head + 1) * head_size] = (
            u * cosine + turned_u * sine
        ).astype(out_ref.dtype)


def project(normed, weight, gain, cosine, sine, rotate):
    rows, width = normed.shape
    cols = weight.shape[1]
    head_size = gain.shape[0]
    tile = min(256, cols)
    row_tile = min(512, rows)
    return pl.pallas_call(
        functools.partial(project_kernel, head_size, rotate),
        out_shape=jax.ShapeDtypeStruct((rows, cols), jnp.bfloat16),
        grid=(cols // tile, rows // row_tile),
        in_specs=[
            pl.BlockSpec((row_tile, width), lambda j, i: (i, 0)),
            pl.BlockSpec((width, tile), lambda j, i: (0, j)),
            pl.BlockSpec((1, head_size), lambda j, i: (0, 0)),
            pl.BlockSpec((row_tile, head_size), lambda j, i: (i, 0)),
            pl.BlockSpec((row_tile, head_size), lambda j, i: (i, 0)),
        ],
        out_specs=pl.BlockSpec((row_tile, tile), lambda j, i: (i, j)),
        compiler_params=pltpu.CompilerParams(vmem_limit_bytes=40 * 1024 * 1024),
        cost_estimate=pl.CostEstimate(
            flops=2 * rows * width * cols,
            bytes_accessed=2 * (rows * width + width * cols + rows * cols),
            transcendentals=0,
        ),
    )(normed, weight, gain[None, :], cosine, sine)


def attend_kernel(head_size, scale, start_ref, q_ref, k_ref, v_ref, out_ref):
    count = q_ref.shape[0]
    span = count + WINDOW_SPAN
    first = pl.multiple_of(start_ref[0] * count, count)
    keys = k_ref[pl.ds(first, span), :]
    values = v_ref[pl.ds(first, span), :]
    row_ids = lax.broadcasted_iota(jnp.int32, (count, span), 0)
    col_ids = lax.broadcasted_iota(jnp.int32, (count, span), 1)
    allowed = (col_ids > row_ids) & (col_ids <= row_ids + WINDOW_SPAN)
    for head in range(q_ref.shape[1] // head_size):
        cols = slice(head * head_size, (head + 1) * head_size)
        scores = lax.dot_general(
            q_ref[:, cols], keys, (((1,), (1,)), ((), ())), preferred_element_type=jnp.float32
        )
        scores = jnp.where(allowed, scores * scale, -jnp.inf)
        highest = jnp.max(scores, axis=-1, keepdims=True)
        weights = jnp.exp(scores - highest)
        total = jnp.sum(weights, axis=-1, keepdims=True)
        mixed = jnp.dot(weights.astype(jnp.bfloat16), values, preferred_element_type=jnp.float32)
        out_ref[:, cols] = (mixed / total).astype(out_ref.dtype)


def attend(start, queries, keys, values, head_size, count, scale):
    rows = keys.shape[0]
    kv_heads = keys.shape[1] // head_size
    group = queries.shape[1] // kv_heads
    span = count + WINDOW_SPAN
    heads = queries.shape[1] // head_size
    return pl.pallas_call(
        functools.partial(attend_kernel, head_size, scale),
        out_shape=jax.ShapeDtypeStruct((count, queries.shape[1]), jnp.bfloat16),
        grid_spec=pltpu.PrefetchScalarGridSpec(
            num_scalar_prefetch=1,
            grid=(kv_heads,),
            in_specs=[
                pl.BlockSpec((count, group), lambda h, s: (s[0], h)),
                pl.BlockSpec((rows, head_size), lambda h, s: (0, h)),
                pl.BlockSpec((rows, head_size), lambda h, s: (0, h)),
            ],
            out_specs=pl.BlockSpec((count, group), lambda h, s: (0, h)),
        ),
        compiler_params=pltpu.CompilerParams(vmem_limit_bytes=24 * 1024 * 1024),
        cost_estimate=pl.CostEstimate(
            flops=8 * heads * count * span * head_size,
            bytes_accessed=4 * rows * keys.shape[1],
            transcendentals=heads * count * span,
        ),
    )(jnp.full((1,), start, jnp.int32), queries, keys, values)


def partner_rows(w_out):
    seq = lax.axis_size("seq")
    seq_index = lax.axis_index("seq")
    rows = w_out.shape[0]
    share = rows // seq
    parts = 2
    piece = share // parts
    got = []
    for part in range(parts):
        mine = lax.dynamic_slice_in_dim(w_out, seq_index * share + part * piece, piece, 0)
        held = swapped(mine, "tp", 1)[None]
        bit = seq // 2
        while bit >= 1:
            other = swapped(held, "seq", bit)
            low = (seq_index & bit) == 0
            held = jnp.concatenate(
                [jnp.where(low, held, other), jnp.where(low, other, held)], axis=0
            )
            bit //= 2
        dims = []
        left = seq
        while left > 1:
            dims.append(2)
            left //= 2
        held = held.reshape(tuple(dims) + (piece, w_out.shape[1]))
        n = len(dims)
        held = held.transpose(tuple(reversed(range(n))) + (n, n + 1))
        got.append(held.reshape(seq, piece, w_out.shape[1]))
    return jnp.stack(got, axis=1).reshape(rows, w_out.shape[1])


def sublayer(
    tokens,
    pre_gain,
    w_query,
    key_weight_matrix,
    value_weight_matrix,
    query_gain,
    key_norm_gain,
    prior_key_cache,
    prior_value_cache,
    w_out,
    post_gain,
):
    seq_tokens = tokens.shape[0]
    tp = lax.axis_size("tp")
    local_rows = seq_tokens // tp
    head_size = query_gain.shape[0]
    seq_index = lax.axis_index("seq")
    tp_index = lax.axis_index("tp")
    side = tp_index % 2
    ring = tp // 2
    place = tp_index // 2
    count = 2 * local_rows

    w_other = partner_rows(w_out)

    normed = root_mean_norm(tokens.astype(jnp.float32), pre_gain).astype(jnp.bfloat16)
    token_positions = WINDOW_SPAN + seq_index * seq_tokens + jnp.arange(seq_tokens, dtype=jnp.int32)
    cosine, sine = rotary_tables(head_size // 2, token_positions)
    cosine = jnp.concatenate([cosine, cosine], axis=1)
    sine = jnp.concatenate([-sine, sine], axis=1)
    key_flat = project(normed, key_weight_matrix, key_norm_gain, cosine, sine, True)
    value_flat = project(normed, value_weight_matrix, key_norm_gain, cosine, sine, False)
    got_keys, got_values = shifted((key_flat, value_flat), "seq", 1)
    queries = project(normed, w_query, query_gain, cosine, sine, True)
    present = seq_index >= 1
    context_keys = jnp.concatenate(
        [jnp.where(present, got_keys, prior_key_cache), key_flat], axis=0
    )
    context_values = jnp.concatenate(
        [jnp.where(present, got_values, prior_value_cache), value_flat], axis=0
    )
    scale = float(MODEL_WIDTH // HQ) ** (-0.5)

    def halves(steps):
        block = (place + steps + ring) % ring
        mixed = attend(block, queries, context_keys, context_values, head_size, count, scale)
        own = lax.dynamic_slice_in_dim(mixed, side * local_rows, local_rows, 0)
        other = lax.dynamic_slice_in_dim(mixed, (1 - side) * local_rows, local_rows, 0)
        return own, other

    def products(distances):
        pairs = [halves(d) for d in distances]
        own = jnp.concatenate([p[0] for p in pairs], axis=0)
        got = swapped(jnp.concatenate([p[1] for p in pairs], axis=0), "tp", 1)
        return jnp.dot(own, w_out, preferred_element_type=jnp.float32) + jnp.dot(
            got, w_other, preferred_element_type=jnp.float32
        )

    middle = w_out.shape[1] // 2
    ahead = behind = None
    far = ring // 2
    if ring % 2 == 0:
        part = products([far]).astype(jnp.bfloat16)
        ahead = turned(part[:, :middle], "tp", 2)
        behind = turned(part[:, middle:], "tp", -2)
        far -= 1
    first = True
    for distance in range(far, 0, -1):
        part = products([distance, -distance])
        up, down = part[:local_rows], part[local_rows:]
        if ahead is not None:
            if first:
                up = jnp.concatenate([up[:, :middle] + ahead, up[:, middle:]], axis=1)
                down = jnp.concatenate([down[:, :middle], down[:, middle:] + behind], axis=1)
            else:
                up = up + ahead
                down = down + behind
        first = False
        ahead = turned(up.astype(jnp.bfloat16), "tp", 2)
        behind = turned(down.astype(jnp.bfloat16), "tp", -2)
    summed = products([0])
    if ahead is not None:
        if ahead.shape[1] != summed.shape[1]:
            summed = summed + jnp.concatenate([ahead, behind], axis=1).astype(jnp.float32)
        else:
            summed = summed + ahead.astype(jnp.float32) + behind.astype(jnp.float32)
    own_rows = lax.dynamic_slice_in_dim(tokens, tp_index * local_rows, local_rows, 0)
    return (own_rows.astype(jnp.float32) + root_mean_norm(summed, post_gain)).astype(jnp.bfloat16)


def solution(mesh):
    return jax.shard_map(
        sublayer,
        mesh=mesh,
        in_specs=(
            P("seq", None),
            P(),
            P(None, "tp"),
            P(None, "tp"),
            P(None, "tp"),
            P(),
            P(),
            P(None, "tp"),
            P(None, "tp"),
            P("tp", None),
            P(),
        ),
        out_specs=P(("seq", "tp"), None),
        check_vma=False,
    )
```

time: 298 us -> 215 us (0.72)
  waiting for transfers between devices: 186 us -> 103 us
  matrix products: 63.6 us -> 11.7 us
  Pallas kernels: 0 us -> 39.5 us
  starting transfers between devices: 7.9 us -> 22.3 us
  between operations: 13.7 us -> 0.52 us
  other arithmetic: 20 us -> 30.6 us
    reduce_scatter x1 -> x0, waiting for transfers between devices: 186 us -> none  [per_device(): lax.psum_scatter(partial_value.astype(jnp.bfloat16), 'tp', scatter_dimens...]
    ppermute x0 -> x13, waiting for transfers between devices: none -> 103 us  [the longest x4 78 us: turned(): lax.ppermute(value, axis, [(source, (source + steps) % count) for source...]
    pallas_call x0 -> x7, Pallas kernels: none -> 39.5 us  [the longest x3 25.8 us: project(): pl.pallas_call(functools.partial(project_kernel, head_size, rotate), out_...]
    dot_general x6, matrix products: 42.8 us -> 11.7 us  [the longest x3 5.98 us: products(): jnp.dot(own, w_out, preferred_element_type=jnp.float32)]
    sub x2 -> x0, matrix products: 20.8 us -> none  [attend_block(): weights = jnp.exp(scores - highest)]
    ppermute x0 -> x13, starting transfers between devices: none -> 15.3 us  [the longest x9 9.08 us: swapped(): lax.ppermute(value, axis, [(source, source ^ bit) for source in range(cou...]
    convert_element_type x2 -> x3, other arithmetic: 3.4 us -> 14.2 us  [the longest x1 11.3 us: sublayer(): root_mean_norm(tokens.astype(jnp.float32), pre_gain).astype(jnp.bfloat16)]
    slice x4 -> x2, local copies, waits for them, and re-layouts: 3.65 us -> 0.2 us  [the longest x1 0.1 us: sublayer(): ahead = turned(part[:, :middle], 'tp', 2)]
  transfers between devices with their start and end apart: 3 -> 15, of which waited for: 1 -> 8; matrix products, arithmetic and copies ran while one was open for 7% -> 17% of each run, Pallas kernels for 0% -> 18%
where the time goes in v1:
time: 215 us
  waiting for transfers between devices  103 us (48%)
  Pallas kernels  39.5 us (18%)
  other arithmetic  30.6 us (14%)
  starting transfers between devices  22.3 us (10%)
  matrix products  11.7 us (5%)
  local copies, waits for them, and re-layouts  6.85 us (3%)
    ppermute x4, waiting for transfers between devices, turned(): lax.ppermute(value, axis, [(source, (source + steps) % count) for source...  78 us
    pallas_call x3, Pallas kernels, project(): pl.pallas_call(functools.partial(project_kernel, head_size, rotate), out_...  25.8 us
    ppermute x9, waiting for transfers between devices, swapped(): lax.ppermute(value, axis, [(source, source ^ bit) for source in range(cou...  25 us
    pallas_call x4, Pallas kernels, attend(): pl.pallas_call(functools.partial(attend_kernel, head_size, scale), out_sh...  13.7 us
    convert_element_type x1, other arithmetic, sublayer(): root_mean_norm(tokens.astype(jnp.float32), pre_gain).astype(jnp.bfloat16)  11.3 us
    ppermute x9, starting transfers between devices, swapped(): lax.ppermute(value, axis, [(source, source ^ bit) for source in range(cou...  9.08 us
    ppermute x2, starting transfers between devices, shifted(): lax.ppermute(value, axis, [(source, source + steps) for source in range(f...  7.04 us
    reduce_sum x1, other arithmetic, root_mean_norm(): mean_square = jnp.mean(values * values, axis=-1, keepdims=True)  6.34 us
  transfers between devices with their start and end apart: 15, of which 8 were waited for; matrix products, arithmetic and copies ran while one was open for 17% of the time, Pallas kernels for 18%

profile of v1, /device:TPU:0, one launch (start us, length us, event | category | flops | bytes accessed | tf_op | source)
XLA Modules:
  0.0 214.5 jit_solution(7980633832520944621)
XLA Ops:
  0.0 2.2 %constant_dynamic-slice_fusion.6 = (bf16[64,5376]{1,0:T(8,128)(2,1)}, bf16[64,5376]{1,0:T(8,128)(2,1)S(1)}) fusion(bf16[512,5376]{1,0:T(8,128)(2,1)} %param.20, s32[]{:T(128)S(6)} %select_n.111, s32[]{:T(128)S(6)} %select_n.116), kind=kLoop, calls=%fused_computation.59 | loop fusion | bytes 2752520 | tf_op jit(solution)/shard_map/dynamic_slice | solution.py:154
  2.2 3.0 %collective-permute-start.3 = (bf16[64,5376]{1,0:T(8,128)(2,1)}, bf16[64,5376]{1,0:T(8,128)(2,1)}, u32[]{:S(2)}, u32[]{:S(2)}) collective-permute-start(bf16[64,5376]{1,0:T(8,128)(2,1)} %get-tuple-element.7), channel_id=1, source_target_pairs={{0,1},{1,0},{2,3},{3,2},{4,5},{5,4},{6,7},{7,6},{8,9},{9,8},{10,11... | collective-permute-start | bytes 2064392 | tf_op jit(solution)/shard_map/ppermute | solution.py:27
  5.3 6.3 %fusion = f32[1024]{0:T(1024)S(1)} fusion(bf16[1024,5376]{1,0:T(8,128)(2,1)} %param.11), kind=kLoop, calls=%fused_computation.2 | loop fusion | flops 16514048 | bytes 11014144 | tf_op jit(solution)/shard_map/reduce_sum | solution.py:38
  11.6 1.9 fusion.12
  13.6 11.3 %fusion.2.x_ref = bf16[1024,5376]{1,0:T(8,128)(2,1)} fusion(bf16[1024,5376]{1,0:T(8,128)(2,1)} %param.11, f32[5376]{0:T(1024)S(1)} %copy-done.10, f32[1024]{0:T(1024)S(1)} %add_rsqrt_fusion), kind=kLoop, calls=%fused_computation.4 | loop fusion | flops 22020096 | bytes 22045696 | tf_op jit(solution)/shard_map/convert_element_type | solution.py:202
  24.9 0.3 pad_maximum_fusion.9
  25.2 7.4 %shard_map.110 = bf16[1024,256]{1,0:T(8,128)(2,1)S(1)} custom-call(bf16[1024,5376]{1,0:T(8,128)(2,1)} %fusion.2.x_ref, bf16[5376,256]{1,0:T(8,128)(2,1)S(1)} %copy-done, f32[1,128]{1,0:T(1,128)S(1)} %bitcast.30, f32[1024,128]{1,0:T(8,128)S(1)} %get-tuple-element.32.cos_ref, f32[1024,128]{1,0:T(8,128)S(1)} %get-tuple-element.33.sin_ref), custom_call_target="tpu_custom_call" | custom-call | flops 2818572288 | bytes 14286848 | tf_op jit(solution)/shard_map/pallas_call | solution.py:74
  32.7 2.7 %collective-permute-start = (bf16[1024,256]{1,0:T(8,128)(2,1)S(1)}, bf16[1024,256]{1,0:T(8,128)(2,1)}, u32[]{:S(2)}, u32[]{:S(2)}) collective-permute-start(bf16[1024,256]{1,0:T(8,128)(2,1)S(1)} %shard_map.110), channel_id=1, source_target_pairs={{0,8},{8,16},{16,24},{1,9},{9,17},{17,25},{2,10},{10,18},{18,26},{... | collective-permute-start | bytes 1572872 | tf_op jit(solution)/shard_map/ppermute | solution.py:22
  35.4 5.8 %shard_map.111 = bf16[1024,256]{1,0:T(8,128)(2,1)S(1)} custom-call(bf16[1024,5376]{1,0:T(8,128)(2,1)} %fusion.2.x_ref, bf16[5376,256]{1,0:T(8,128)(2,1)S(1)} %copy-done.1, f32[1,128]{1,0:T(1,128)S(1)} %bitcast.31, f32[1024,128]{1,0:T(8,128)S(1)} %get-tuple-element.32.cos_ref, f32[1024,128]{1,0:T(8,128)S(1)} %get-tuple-element.33.sin_ref), custom_call_target="tpu_custom_call" | custom-call | flops 2818572288 | bytes 14286848 | tf_op jit(solution)/shard_map/pallas_call | solution.py:74
  41.2 4.3 %collective-permute-start.1 = (bf16[1024,256]{1,0:T(8,128)(2,1)S(1)}, bf16[1024,256]{1,0:T(8,128)(2,1)}, u32[]{:S(2)}, u32[]{:S(2)}) collective-permute-start(bf16[1024,256]{1,0:T(8,128)(2,1)S(1)} %shard_map.111), channel_id=1, source_target_pairs={{0,8},{8,16},{16,24},{1,9},{9,17},{17,25},{2,10},{10,18},{18,26},{... | collective-permute-start | bytes 1572872 | tf_op jit(solution)/shard_map/ppermute | solution.py:22
  45.6 12.5 %shard_map.109.q_ref = bf16[1024,512]{1,0:T(8,128)(2,1)S(1)} custom-call(bf16[1024,5376]{1,0:T(8,128)(2,1)} %fusion.2.x_ref, bf16[5376,512]{1,0:T(8,128)(2,1)S(1)} %bitcast.33, f32[1,128]{1,0:T(1,128)S(1)} %bitcast.34, f32[1024,128]{1,0:T(8,128)S(1)} %get-tuple-element.32.cos_ref, f32[1024,128]{1,0:T(8,128)S(1)} %get-tuple-element.33.sin_ref), custom_call_target="tpu_custom_call" | custom-call | flops 5637144576 | bytes 17563648 | tf_op jit(solution)/shard_map/pallas_call | solution.py:74
  58.2 1.0 copy-done.4
  59.5 1.0 copy-done.5
  60.4 3.4 %shard_map.115 = bf16[256,512]{1,0:T(8,128)(2,1)S(1)} custom-call(s32[1]{0:T(128)} %bitcast.14.start_ref, bf16[1024,512]{1,0:T(8,128)(2,1)S(1)} %copy-done.5, bf16[2048,256]{1,0:T(8,128)(2,1)S(1)} %pad_maximum_fusion.7.k_ref, bf16[2048,256]{1,0:T(8,128)(2,1)S(1)} %pad_maximum_fusion.8.v_ref), custom_call_target="tpu_custom_call" | custom-call | flops 1342177280 | bytes 2097152 | tf_op jit(solution)/shard_map/pallas_call | solution.py:123
  63.8 1.6 collective-permute-start.10
  65.4 0.6 collective-permute-start.4
  66.0 1.5 collective-permute-start.7
  67.4 3.4 %shard_map.113 = bf16[256,512]{1,0:T(8,128)(2,1)S(1)} custom-call(s32[1]{0:T(128)} %bitcast.12.start_ref, bf16[1024,512]{1,0:T(8,128)(2,1)S(1)} %copy-done.5, bf16[2048,256]{1,0:T(8,128)(2,1)S(1)} %pad_maximum_fusion.7.k_ref, bf16[2048,256]{1,0:T(8,128)(2,1)S(1)} %pad_maximum_fusion.8.v_ref), custom_call_target="tpu_custom_call" | custom-call | flops 1342177280 | bytes 2097152 | tf_op jit(solution)/shard_map/pallas_call | solution.py:123
  70.8 3.6 %shard_map.114 = bf16[256,512]{1,0:T(8,128)(2,1)S(1)} custom-call(s32[1]{0:T(128)} %bitcast.13.start_ref, bf16[1024,512]{1,0:T(8,128)(2,1)S(1)} %copy-done.5, bf16[2048,256]{1,0:T(8,128)(2,1)S(1)} %pad_maximum_fusion.7.k_ref, bf16[2048,256]{1,0:T(8,128)(2,1)S(1)} %pad_maximum_fusion.8.v_ref), custom_call_target="tpu_custom_call" | custom-call | flops 1342177280 | bytes 2097152 | tf_op jit(solution)/shard_map/pallas_call | solution.py:123
  74.5 0.9 fusion.13
  75.4 8.5 %collective-permute-done.4 = bf16[1,64,5376]{2,1,0:T(8,128)(2,1)S(1)} collective-permute-done((bf16[1,64,5376]{2,1,0:T(8,128)(2,1)}, bf16[1,64,5376]{2,1,0:T(8,128)(2,1)S(1)}, u32[]{:S(2)}, u32[]{:S(2)}) %collective-permute-start.4) | collective-permute-done | bytes 688160 | tf_op jit(solution)/shard_map/ppermute | solution.py:27
  83.9 14.2 %collective-permute-done.7 = bf16[1,64,5376]{2,1,0:T(8,128)(2,1)S(1)} collective-permute-done((bf16[1,64,5376]{2,1,0:T(8,128)(2,1)}, bf16[1,64,5376]{2,1,0:T(8,128)(2,1)S(1)}, u32[]{:S(2)}, u32[]{:S(2)}) %collective-permute-start.7) | collective-permute-done | bytes 688160 | tf_op jit(solution)/shard_map/ppermute | solution.py:27
  98.1 1.5 broadcast_select_fusion.5
  99.9 0.6 collective-permute-start.9
  100.5 1.6 fusion.8
  102.2 0.3 collective-permute-start.8
  102.5 0.4 collective-permute-done.5
  103.6 1.9 collective-permute-done.8
  105.8 1.7 copy.13
  107.6 2.3 %pad_maximum_fusion = bf16[4,2,64,5376]{3,2,0,1:T(8,128)(2,1)S(1)} fusion(bf16[4,1,64,5376]{3,2,0,1:T(8,128)(2,1)} %bitcast.45, bf16[4,1,64,5376]{3,2,0,1:T(8,128)(2,1)S(1)} %bitcast.42), kind=kLoop, calls=%fused_computation.11 | loop fusion | flops 2752512 | bytes 11010048 | tf_op jit(solution)/shard_map/stack | solution.py:173
  109.8 0.4 copy.14
  110.3 0.9 fusion.5
  111.3 1.6 collective-permute-start.11
  113.0 2.2 %collective-permute-start.13 = (bf16[128,2688]{1,0:T(8,128)(2,1)S(1)}, bf16[128,2688]{1,0:T(8,128)(2,1)S(1)}, u32[]{:S(2)}, u32[]{:S(2)}) collective-permute-start(bf16[128,2688]{1,0:T(8,128)(2,1)S(1)} %get-tuple-element.16), channel_id=1, source_target_pairs={{0,6},{1,7},{2,0},{3,1},{4,2},{5,3},{6,4},{7,5},{8,14},{9,15},{10,... | collective-permute-start | bytes 2064392 | tf_op jit(solution)/shard_map/ppermute | solution.py:32
  115.2 1.6 fusion.22
  116.9 14.6 %collective-permute-done.11 = bf16[128,2688]{1,0:T(8,128)(2,1)S(1)} collective-permute-done((bf16[128,2688]{1,0:T(8,128)(2,1)S(1)}, bf16[128,2688]{1,0:T(8,128)(2,1)S(1)}, u32[]{:S(2)}, u32[]{:S(2)}) %collective-permute-start.11) | collective-permute-done | bytes 688160 | tf_op jit(solution)/shard_map/ppermute | solution.py:32
  131.5 13.4 %collective-permute-done.13 = bf16[128,2688]{1,0:T(8,128)(2,1)S(1)} collective-permute-done((bf16[128,2688]{1,0:T(8,128)(2,1)S(1)}, bf16[128,2688]{1,0:T(8,128)(2,1)S(1)}, u32[]{:S(2)}, u32[]{:S(2)}) %collective-permute-start.13) | collective-permute-done | bytes 688160 | tf_op jit(solution)/shard_map/ppermute | solution.py:32
  145.0 0.2 fusion.7
  145.2 1.2 pad_maximum_fusion.6
  146.4 2.3 %collective-permute-start.14 = (bf16[128,5376]{1,0:T(8,128)(2,1)}, bf16[128,5376]{1,0:T(8,128)(2,1)}, u32[]{:S(2)}, u32[]{:S(2)}) collective-permute-start(bf16[128,5376]{1,0:T(8,128)(2,1)} %pad_maximum_fusion.6), channel_id=1, source_target_pairs={{0,6},{1,7},{2,0},{3,1},{4,2},{5,3},{6,4},{7,5},{8,14},{9,15},{10,... | collective-permute-start | bytes 4128776 | tf_op jit(solution)/shard_map/ppermute | solution.py:32
  148.7 1.2 pad_maximum_fusion.5
  149.9 3.4 %shard_map.112 = bf16[256,512]{1,0:T(8,128)(2,1)S(1)} custom-call(s32[1]{0:T(128)} %bitcast.start_ref, bf16[1024,512]{1,0:T(8,128)(2,1)S(1)} %copy-done.6, bf16[2048,256]{1,0:T(8,128)(2,1)S(1)} %pad_maximum_fusion.7.k_ref, bf16[2048,256]{1,0:T(8,128)(2,1)S(1)} %pad_maximum_fusion.8.v_ref), custom_call_target="tpu_custom_call" | custom-call | flops 1342177280 | bytes 2097152 | tf_op jit(solution)/shard_map/pallas_call | solution.py:123
  153.3 1.6 collective-permute-start.2
  154.9 3.5 %fusion.15 = f32[128,5376]{1,0:T(8,128)S(1)} fusion(bf16[512,5376]{1,0:T(8,128)(2,1)} %param.20, bf16[256,512]{1,0:T(8,128)(2,1)S(1)} %shard_map.112, s32[]{:T(128)S(6)} %select_n.107), kind=kOutput, calls=%fused_computation.48 | convolution fusion | flops 704643072 | bytes 8388612 | tf_op jit(solution)/shard_map/dot_general | solution.py:231
  158.4 21.3 %collective-permute-done.14 = bf16[128,5376]{1,0:T(8,128)(2,1)} collective-permute-done((bf16[128,5376]{1,0:T(8,128)(2,1)}, bf16[128,5376]{1,0:T(8,128)(2,1)}, u32[]{:S(2)}, u32[]{:S(2)}) %collective-permute-start.14) | collective-permute-done | bytes 1376288 | tf_op jit(solution)/shard_map/ppermute | solution.py:32
  179.7 28.7 %collective-permute-done.12 = bf16[128,5376]{1,0:T(8,128)(2,1)} collective-permute-done((bf16[128,5376]{1,0:T(8,128)(2,1)}, bf16[128,5376]{1,0:T(8,128)(2,1)}, u32[]{:S(2)}, u32[]{:S(2)}) %collective-permute-start.12) | collective-permute-done | bytes 1376288 | tf_op jit(solution)/shard_map/ppermute | solution.py:32
  208.4 3.2 %multiply_reduce_fusion = (f32[128]{0:T(128)S(1)}, f32[128,5376]{1,0:T(8,128)S(1)}) fusion(bf16[128,5376]{1,0:T(8,128)(2,1)} %collective-permute-done.14, bf16[128,5376]{1,0:T(8,128)(2,1)} %collective-permute-done.12, f32[128,5376]{1,0:T(8,128)S(1)} %fusion.15, bf16[128,512]{1,0:T(8,128)(2,1)S(1)} %collective-permute-done.2, bf16[512,5376]{1,0:T(8,128)(2,1)S(1)} %bitcast.39), kind=kOutput, calls=%fused_computation.15 | convolution fusion | flops 709459840 | bytes 13894144 | tf_op jit(solution)/shard_map/dot_general | solution.py:231
  211.6 2.9 %add_convert_fusion = bf16[128,5376]{1,0:T(8,128)(2,1)} fusion(f32[128,5376]{1,0:T(8,128)S(1)} %get-tuple-element.31, f32[5376]{0:T(1024)S(1)} %copy-done.11, f32[128]{0:T(128)S(1)} %add_rsqrt_fusion.1, bf16[1024,5376]{1,0:T(8,128)(2,1)} %param.11, s32[]{:T(128)S(6)} %select_n.100), kind=kLoop, calls=%fused_computation.14 | loop fusion | flops 3440640 | bytes 5527044 | tf_op jit(solution)/shard_map/convert_element_type | solution.py:264
  (69 shorter events, 2.1 us)
Async XLA Ops:
  2.2 63.1 %collective-permute-start.3 = (bf16[64,5376]{1,0:T(8,128)(2,1)}, bf16[64,5376]{1,0:T(8,128)(2,1)}, u32[]{:S(2)}, u32[]{:S(2)}) collective-permute-start(bf16[64,5376]{1,0:T(8,128)(2,1)} %get-tuple-element.7), channel_id=1, source_target_pairs={{0,1},{1,0},{2,3},{3,2},{4,5},{5,4},{6,7},{7,6},{8,9},{9,8},{10,11... | collective-permute-start | bytes 2064392 | tf_op jit(solution)/shard_map/ppermute | solution.py:27
  5.2 60.7 %collective-permute-start.6 = (bf16[64,5376]{1,0:T(8,128)(2,1)S(1)}, bf16[64,5376]{1,0:T(8,128)(2,1)}, u32[]{:S(2)}, u32[]{:S(2)}) collective-permute-start(bf16[64,5376]{1,0:T(8,128)(2,1)S(1)} %get-tuple-element.8), channel_id=1, source_target_pairs={{0,1},{1,0},{2,3},{3,2},{4,5},{5,4},{6,7},{7,6},{8,9},{9,8},{10,11... | collective-permute-start | bytes 2064392 | tf_op jit(solution)/shard_map/ppermute | solution.py:27
  5.3 8.3 %copy-start.10 = (f32[5376]{0:T(1024)S(1)}, f32[5376]{0:T(1024)}, u32[]{:S(2)}) copy-start(f32[5376]{0:T(1024)} %param.12) | copy-start | bytes 64516
  13.5 11.7 %copy-start = (bf16[5376,256]{1,0:T(8,128)(2,1)S(1)}, bf16[5376,256]{1,0:T(8,128)(2,1)}, u32[]{:S(2)}) copy-start(bf16[5376,256]{1,0:T(8,128)(2,1)} %w_ref.4) | copy-start | bytes 8257540
  13.5 11.7 %copy-start.2 = (f32[128]{0:T(128)S(1)}, f32[128]{0:T(128)}, u32[]{:S(2)}) copy-start(f32[128]{0:T(128)} %param.17) | copy-start | bytes 1540
  25.2 10.2 %copy-start.1 = (bf16[5376,256]{1,0:T(8,128)(2,1)S(1)}, bf16[5376,256]{1,0:T(8,128)(2,1)}, u32[]{:S(2)}) copy-start(bf16[5376,256]{1,0:T(8,128)(2,1)} %w_ref.5) | copy-start | bytes 8257540
  25.2 20.3 %slice-start = ((s8[5505024]{0:T(1024)(128)(4,1)}), s8[1310720]{0:T(1024)(128)(4,1)S(1)}, s32[]{:S(2)}) async-start(s8[5505024]{0:T(1024)(128)(4,1)} %bitcast.32), calls=%async_computation | async-start | bytes 2621440
  32.7 12.9 %slice-start.1 = ((s8[5505024]{0:T(1024)(128)(4,1)}), s8[4194304]{0:T(1024)(128)(4,1)S(1)}, s32[]{:S(2)}) async-start(s8[5505024]{0:T(1024)(128)(4,1)} %bitcast.32), calls=%async_computation.1 | async-start | bytes 8388608
  32.7 12.9 %copy-start.3 = (f32[128]{0:T(128)S(1)}, f32[128]{0:T(128)}, u32[]{:S(2)}) copy-start(f32[128]{0:T(128)} %param.16) | copy-start | bytes 1540
  32.7 26.4 %collective-permute-start = (bf16[1024,256]{1,0:T(8,128)(2,1)S(1)}, bf16[1024,256]{1,0:T(8,128)(2,1)}, u32[]{:S(2)}, u32[]{:S(2)}) collective-permute-start(bf16[1024,256]{1,0:T(8,128)(2,1)S(1)} %shard_map.110), channel_id=1, source_target_pairs={{0,8},{8,16},{16,24},{1,9},{9,17},{17,25},{2,10},{10,18},{18,26},{... | collective-permute-start | bytes 1572872 | tf_op jit(solution)/shard_map/ppermute | solution.py:22
  41.2 18.0 %collective-permute-start.1 = (bf16[1024,256]{1,0:T(8,128)(2,1)S(1)}, bf16[1024,256]{1,0:T(8,128)(2,1)}, u32[]{:S(2)}, u32[]{:S(2)}) collective-permute-start(bf16[1024,256]{1,0:T(8,128)(2,1)S(1)} %shard_map.111), channel_id=1, source_target_pairs={{0,8},{8,16},{16,24},{1,9},{9,17},{17,25},{2,10},{10,18},{18,26},{... | collective-permute-start | bytes 1572872 | tf_op jit(solution)/shard_map/ppermute | solution.py:22
  45.6 13.5 %copy-start.8 = (bf16[1024,256]{1,0:T(8,128)(2,1)S(1)}, bf16[1024,256]{1,0:T(8,128)(2,1)}, u32[]{:S(2)}) copy-start(bf16[1024,256]{1,0:T(8,128)(2,1)} %param.18) | copy-start | bytes 1572868
  45.6 13.6 %copy-start.9 = (bf16[1024,256]{1,0:T(8,128)(2,1)S(1)}, bf16[1024,256]{1,0:T(8,128)(2,1)}, u32[]{:S(2)}) copy-start(bf16[1024,256]{1,0:T(8,128)(2,1)} %param.19) | copy-start | bytes 1572868
  58.1 1.0 copy-start.4
  59.2 1.2 copy-start.5
  60.4 14.0 %slice-start.4 = ((s8[5505024]{0:T(1024)(128)(4,1)}), s8[4194304]{0:T(1024)(128)(4,1)S(1)}, s32[]{:S(2)}) async-start(s8[5505024]{0:T(1024)(128)(4,1)} %bitcast.40), calls=%async_computation.4 | async-start | bytes 8388608
  63.8 46.5 %collective-permute-start.10 = (bf16[128,512]{1,0:T(8,128)(2,1)S(1)}, bf16[128,512]{1,0:T(8,128)(2,1)S(1)}, u32[]{:S(2)}, u32[]{:S(2)}) collective-permute-start(bf16[128,512]{1,0:T(8,128)(2,1)S(1)} %constant_dynamic-slice_fusion), channel_id=1, source_target_pairs={{0,1},{1,0},{2,3},{3,2},{4,5},{5,4},{6,7},{7,6},{8,9},{9,8},{10,11... | collective-permute-start | bytes 393224 | tf_op jit(solution)/shard_map/ppermute | solution.py:27
  65.4 18.5 %collective-permute-start.4 = (bf16[1,64,5376]{2,1,0:T(8,128)(2,1)}, bf16[1,64,5376]{2,1,0:T(8,128)(2,1)S(1)}, u32[]{:S(2)}, u32[]{:S(2)}) collective-permute-start(bf16[1,64,5376]{2,1,0:T(8,128)(2,1)} %bitcast.3), channel_id=1, source_target_pairs={{0,16},{8,24},{16,0},{24,8},{1,17},{9,25},{17,1},{25,9},{2,18},{10... | collective-permute-start | bytes 2064392 | tf_op jit(solution)/shard_map/ppermute | solution.py:27
  66.0 32.1 %collective-permute-start.7 = (bf16[1,64,5376]{2,1,0:T(8,128)(2,1)}, bf16[1,64,5376]{2,1,0:T(8,128)(2,1)S(1)}, u32[]{:S(2)}, u32[]{:S(2)}) collective-permute-start(bf16[1,64,5376]{2,1,0:T(8,128)(2,1)} %bitcast.7), channel_id=1, source_target_pairs={{0,16},{8,24},{16,0},{24,8},{1,17},{9,25},{17,1},{25,9},{2,18},{10... | collective-permute-start | bytes 2064392 | tf_op jit(solution)/shard_map/ppermute | solution.py:27
  67.4 7.0 %slice-start.5 = ((s8[5505024]{0:T(1024)(128)(4,1)}), s8[1310720]{0:T(1024)(128)(4,1)S(1)}, s32[]{:S(2)}) async-start(s8[5505024]{0:T(1024)(128)(4,1)} %bitcast.40), calls=%async_computation.5 | async-start | bytes 2621440
  99.7 3.2 %collective-permute-start.5 = (bf16[2,64,5376]{2,1,0:T(8,128)(2,1)S(1)}, bf16[2,64,5376]{2,1,0:T(8,128)(2,1)S(1)}, u32[]{:S(2)}, u32[]{:S(2)}) collective-permute-start(bf16[2,64,5376]{2,1,0:T(8,128)(2,1)S(1)} %pad_maximum_fusion.3), channel_id=1, source_target_pairs={{0,8},{8,0},{16,24},{24,16},{1,9},{9,1},{17,25},{25,17},{2,10},{10... | collective-permute-start | bytes 4128776 | tf_op jit(solution)/shard_map/ppermute | solution.py:27
  99.9 15.3 %collective-permute-start.9 = (bf16[256,512]{1,0:T(8,128)(2,1)S(1)}, bf16[256,512]{1,0:T(8,128)(2,1)S(1)}, u32[]{:S(2)}, u32[]{:S(2)}) collective-permute-start(bf16[256,512]{1,0:T(8,128)(2,1)S(1)} %pad_maximum_fusion.11), channel_id=1, source_target_pairs={{0,1},{1,0},{2,3},{3,2},{4,5},{5,4},{6,7},{7,6},{8,9},{9,8},{10,11... | collective-permute-start | bytes 786440 | tf_op jit(solution)/shard_map/ppermute | solution.py:27
  102.2 3.2 %collective-permute-start.8 = (bf16[2,64,5376]{2,1,0:T(8,128)(2,1)S(1)}, bf16[2,64,5376]{2,1,0:T(8,128)(2,1)S(1)}, u32[]{:S(2)}, u32[]{:S(2)}) collective-permute-start(bf16[2,64,5376]{2,1,0:T(8,128)(2,1)S(1)} %pad_maximum_fusion.4), channel_id=1, source_target_pairs={{0,8},{8,0},{16,24},{24,16},{1,9},{9,1},{17,25},{25,17},{2,10},{10... | collective-permute-start | bytes 4128776 | tf_op jit(solution)/shard_map/ppermute | solution.py:27
  110.3 4.9 %copy-start.7 = (bf16[4,2,64,5376]{3,2,1,0:T(8,128)(2,1)}, bf16[4,2,64,5376]{3,2,1,0:T(8,128)(2,1)S(1)}, u32[]{:S(2)}) copy-start(bf16[4,2,64,5376]{3,2,1,0:T(8,128)(2,1)S(1)} %copy.14) | copy-start | bytes 16515076
  111.3 20.2 %collective-permute-start.11 = (bf16[128,2688]{1,0:T(8,128)(2,1)S(1)}, bf16[128,2688]{1,0:T(8,128)(2,1)S(1)}, u32[]{:S(2)}, u32[]{:S(2)}) collective-permute-start(bf16[128,2688]{1,0:T(8,128)(2,1)S(1)} %get-tuple-element.15), channel_id=1, source_target_pairs={{0,2},{1,3},{2,4},{3,5},{4,6},{5,7},{6,0},{7,1},{8,10},{9,11},{10,... | collective-permute-start | bytes 2064392 | tf_op jit(solution)/shard_map/ppermute | solution.py:32
  113.0 32.0 %collective-permute-start.13 = (bf16[128,2688]{1,0:T(8,128)(2,1)S(1)}, bf16[128,2688]{1,0:T(8,128)(2,1)S(1)}, u32[]{:S(2)}, u32[]{:S(2)}) collective-permute-start(bf16[128,2688]{1,0:T(8,128)(2,1)S(1)} %get-tuple-element.16), channel_id=1, source_target_pairs={{0,6},{1,7},{2,0},{3,1},{4,2},{5,3},{6,4},{7,5},{8,14},{9,15},{10,... | collective-permute-start | bytes 2064392 | tf_op jit(solution)/shard_map/ppermute | solution.py:32
  145.2 4.7 %copy-start.6 = (bf16[1024,512]{1,0:T(8,128)(2,1)S(1)}, bf16[1024,512]{1,0:T(8,128)(2,1)}, u32[]{:S(2)}) copy-start(bf16[1024,512]{1,0:T(8,128)(2,1)} %copy-done.4) | copy-start | bytes 3145732
  146.4 33.3 %collective-permute-start.14 = (bf16[128,5376]{1,0:T(8,128)(2,1)}, bf16[128,5376]{1,0:T(8,128)(2,1)}, u32[]{:S(2)}, u32[]{:S(2)}) collective-permute-start(bf16[128,5376]{1,0:T(8,128)(2,1)} %pad_maximum_fusion.6), channel_id=1, source_target_pairs={{0,6},{1,7},{2,0},{3,1},{4,2},{5,3},{6,4},{7,5},{8,14},{9,15},{10,... | collective-permute-start | bytes 4128776 | tf_op jit(solution)/shard_map/ppermute | solution.py:32
  149.9 58.5 %collective-permute-start.12 = (bf16[128,5376]{1,0:T(8,128)(2,1)}, bf16[128,5376]{1,0:T(8,128)(2,1)}, u32[]{:S(2)}, u32[]{:S(2)}) collective-permute-start(bf16[128,5376]{1,0:T(8,128)(2,1)} %pad_maximum_fusion.5), channel_id=1, source_target_pairs={{0,2},{1,3},{2,4},{3,5},{4,6},{5,7},{6,0},{7,1},{8,10},{9,11},{10,... | collective-permute-start | bytes 4128776 | tf_op jit(solution)/shard_map/ppermute | solution.py:32
  153.3 55.1 %slice-start.2 = ((s8[5505024]{0:T(1024)(128)(4,1)}), s8[4194304]{0:T(1024)(128)(4,1)S(1)}, s32[]{:S(2)}) async-start(s8[5505024]{0:T(1024)(128)(4,1)} %bitcast.37), calls=%async_computation.2 | async-start | bytes 8388608
  153.3 55.1 %slice-start.3 = ((s8[5505024]{0:T(1024)(128)(4,1)}), s8[1310720]{0:T(1024)(128)(4,1)S(1)}, s32[]{:S(2)}) async-start(s8[5505024]{0:T(1024)(128)(4,1)} %bitcast.37), calls=%async_computation.3 | async-start | bytes 2621440
  153.3 5.1 %collective-permute-start.2 = (bf16[128,512]{1,0:T(8,128)(2,1)S(1)}, bf16[128,512]{1,0:T(8,128)(2,1)S(1)}, u32[]{:S(2)}, u32[]{:S(2)}) collective-permute-start(bf16[128,512]{1,0:T(8,128)(2,1)S(1)} %constant_dynamic-slice_fusion.7), channel_id=1, source_target_pairs={{0,1},{1,0},{2,3},{3,2},{4,5},{5,4},{6,7},{7,6},{8,9},{9,8},{10,11... | collective-permute-start | bytes 393224 | tf_op jit(solution)/shard_map/ppermute | solution.py:27
  158.4 53.2 %copy-start.11 = (f32[5376]{0:T(1024)S(1)}, f32[5376]{0:T(1024)}, u32[]{:S(2)}) copy-start(f32[5376]{0:T(1024)} %param.21) | copy-start | bytes 64516
